TPU v7x, 256 devices: a whole 4x4x8 slice. The times are simulated.
256 devices in a mesh: blk: 128 (over x, z, y), rep: 2 (over core).
Axes of the slice: x: 4, y: 4, z: 8, core: 2. Of those that a mesh axis runs over, the one named last changes fastest.
Arguments:
- item_factors: bfloat16 [262144, 256], P('blk')
- user_factors: float32 [2048, 256], P(('blk', 'rep'))
- item_lists: int32 [2048, 128], P(('blk', 'rep')), may hold values from 0 to 262143, as said below
- counts: int32 [2048], P(('blk', 'rep')), may hold values from 16 to 112, as said below
- plays: int32 [2048, 128], P(('blk', 'rep')), may hold values from 0 to 999
Outputs:
- new_factors: float32 [2048, 256], P(('blk', 'rep'))
- residual_norms: float32 [4], replicated
Inputs may be any that keep to these rules, and one draw needn't show every extreme that they name: `item_lists`: entries are global item rows; index b of blk holds rows b * 2048 to (b + 1) * 2048 - 1. Among the live slots of the users of one device, at most 8 name rows held by one index of blk, and in every draw some index of blk is named by exactly 8 live slots of every device. The padding slots of one device name rows of every index of blk exactly 4 times. Slots at or after counts[u] are padding. The 8 users of one device have 8 * 64 live slots in all.
All inputs are finite; a program needn't handle non-finite values.
Results may differ from a plain program's by a relative error of at most 0.0003.
Values may be sent and summed in bfloat16 or wider, within the bound.
A program may use at most 64 MiB of HBM per device.

v0:
```python
import jax
import jax.numpy as jnp
from jax import lax
from jax.sharding import Mesh
from jax.sharding import PartitionSpec as P

ITERS = 3
BLK_REP = ("blk_0", "blk_1", "blk_2", "rep")
BLK = ("blk_0", "blk_1", "blk_2")
conf_scale = 40.0
ridge = 1.0
tiny = 1e-06


def over_axes(array, axes):
    for axis in axes:
        array = lax.psum(array, axis)
    return array


def split_up(array, dim, devices):
    dims = array.shape
    pieces = array.reshape(*dims[:dim], devices, dims[dim] // devices, *dims[dim + 1 :])
    return jnp.moveaxis(pieces, dim, 0)


def laid_out(pieces, dim):
    dims = list(pieces.shape[1:])
    dims[dim] *= pieces.shape[0]
    return jnp.moveaxis(pieces, 0, dim).reshape(dims)


def moved_by_axis(pieces, axes, sequence):
    dims = [lax.axis_size(a) for a in axes]
    pieces = pieces.reshape(*dims, *pieces.shape[1:])
    for k in sequence:
        pieces = lax.all_to_all(pieces, axes[k], split_axis=k, concat_axis=k, tiled=True)
    return pieces.reshape(-1, *pieces.shape[len(axes) :])


def exchange_by_axis(array, axes, sequence, split_dim, concat_dim):
    pieces = split_up(array, split_dim, lax.axis_size(axes))
    return laid_out(moved_by_axis(pieces, axes, sequence), concat_dim)


def operator_apply(vector, gram, item_rows, extra_weight):
    along = jnp.einsum(
        "ulk,uk->ul",
        item_rows,
        vector,
        precision=lax.Precision.HIGHEST,
        preferred_element_type=jnp.float32,
    )
    back = jnp.einsum(
        "ul,ulk->uk",
        extra_weight * along,
        item_rows,
        precision=lax.Precision.HIGHEST,
        preferred_element_type=jnp.float32,
    )
    return jnp.dot(vector, gram, precision=lax.Precision.HIGHEST) + back + ridge * vector


def global_squares(value):
    return over_axes(value, BLK_REP)


def pack_requests(owner_key, local, blocks, capacity):
    slot_total = owner_key.shape[0]
    order = jnp.argsort(owner_key, stable=True)
    sorted_owner = owner_key[order]
    starts = jnp.searchsorted(sorted_owner, jnp.arange(blocks + 1, dtype=jnp.int32))
    rank_sorted = jnp.arange(slot_total, dtype=jnp.int32) - starts[sorted_owner]
    place_sorted = jnp.where(
        sorted_owner < blocks, sorted_owner * capacity + rank_sorted, blocks * capacity
    )
    place = jnp.zeros((slot_total,), jnp.int32).at[order].set(place_sorted)
    requests = jnp.zeros((blocks * capacity + 1,), jnp.int32).at[place].set(local)
    requests = requests[: blocks * capacity].reshape(blocks, capacity)
    return (requests, jnp.minimum(place, blocks * capacity - 1))


def body(item_factors, user_factors, item_lists, counts, plays):
    own_rows, width = item_factors.shape
    user_count, list_len = item_lists.shape
    blocks = lax.axis_size(BLK)
    slot_total = user_count * list_len
    half_rows = own_rows // lax.axis_size("rep")
    mine = lax.dynamic_slice_in_dim(item_factors, lax.axis_index("rep") * half_rows, half_rows, 0)
    partial_gram = lax.dot_general(
        mine, mine, (((0,), (0,)), ((), ())), preferred_element_type=jnp.float32
    )
    gram = over_axes(partial_gram, BLK_REP)
    live = jnp.arange(list_len, dtype=jnp.int32)[None, :] < counts[:, None]
    flat_ids = item_lists.reshape(slot_total)
    owner = flat_ids // own_rows
    local = flat_ids % own_rows
    capacity = 3 * slot_total // (2 * blocks)
    requests, place = pack_requests(owner, local, blocks, capacity)
    found = item_factors[exchange_by_axis(requests, BLK, (0, 1, 2), 0, 0)]
    reply = lax.all_to_all(found, BLK, split_axis=0, concat_axis=0, tiled=True)
    item_rows = reply.reshape(blocks * capacity, width)[place].reshape(user_count, list_len, width)
    confidence = 1.0 + conf_scale * jnp.log(2.0 + plays.astype(jnp.float32))
    full_weight = jnp.where(live, confidence, jnp.float32(0.0))
    extra_weight = jnp.where(live, confidence - 1.0, jnp.float32(0.0))
    target = jnp.einsum(
        "ul,ulk->uk",
        full_weight,
        item_rows,
        precision=lax.Precision.HIGHEST,
        preferred_element_type=jnp.float32,
    )
    solution = user_factors
    residual = target - operator_apply(solution, gram, item_rows, extra_weight)
    direction = residual
    squares = jnp.sum(residual * residual, axis=1)
    collected = [jnp.sum(squares)]
    for _ in range(ITERS):
        image = operator_apply(direction, gram, item_rows, extra_weight)
        alpha = squares / (jnp.sum(direction * image, axis=1) + tiny)
        solution = solution + alpha[:, None] * direction
        residual = residual - alpha[:, None] * image
        fresh = jnp.sum(residual * residual, axis=1)
        direction = residual + (fresh / (squares + tiny))[:, None] * direction
        squares = fresh
        collected.append(jnp.sum(squares))
    totals = jnp.stack([global_squares(value) for value in collected])
    users_total = user_count * lax.axis_size(BLK) * lax.axis_size("rep")
    return (solution, jnp.sqrt(totals / (users_total * width)))


def solution(mesh):
    split = Mesh(
        mesh.devices.reshape(4, 8, 4, mesh.shape["rep"]), ("blk_0", "blk_1", "blk_2", "rep")
    )
    in_specs = (P(BLK, None), P(BLK_REP, None), P(BLK_REP, None), P(BLK_REP), P(BLK_REP, None))
    out_specs = (P(BLK_REP, None), P())
    return jax.shard_map(body, mesh=split, in_specs=in_specs, out_specs=out_specs, check_vma=False)
```

profile of v0, /device:TPU:1, one launch (start us, length us, event | category | flops | bytes accessed | tf_op | source)
XLA Modules:
  0.0 366.3 jit_solution(18274535382460058586)
XLA Ops:
  8.0 4.4 %sort.17 = (s32[1024]{0:T(1024)}, s32[1024]{0:T(1024)S(1)}) sort(s32[1024]{0:T(1024)S(1)} %get-tuple-element.128, s32[1024]{0:T(1024)S(1)} %iota.14), dimensions={0}, to_apply=%region_0.0 | sort | flops 10240 | bytes 16384 | tf_op jit(solution)/shard_map/jit(argsort)/sort | solution.py:70
  12.4 4.5 %gather_fusion.1 = s32[1024]{0:T(1024)S(1)} fusion(s32[1024]{0:T(1024)S(1)} %get-tuple-element.128, s32[1024]{0:T(1024)S(1)} %get-tuple-element.129), kind=kCustom, calls=%fused_computation.1 | custom fusion | bytes 12288 | tf_op jit(solution)/shard_map/gather | solution.py:71
  16.9 13.7 %while.24 = (s32[]{:T(128)}, u32[129]{0:T(256)S(1)}, u32[129]{0:T(256)S(1)}, s32[1024]{0:T(1024)S(1)}, s32[]{:T(128)}, /*index=5*/s32[]{:T(128)}, s32[]{}) while((s32[]{:T(128)}, u32[129]{0:T(256)S(1)}, u32[129]{0:T(256)S(1)}, s32[1024]{0:T(1024)S(1)}, s32[]{:T(128)}, /*index=5*/s32[]{:T(128)}, s32[]{}) %tuple.51), condition=%wide.region_2.0_spmd.clone, body=%wide.region_1.0_spmd.clone.sunk | while | flops 2705 | bytes 10388 | solution.py:72
  17.0 1.2 gather_fusion
  18.2 1.2 gather_fusion
  19.4 1.2 gather_fusion
  20.7 1.2 gather_fusion
  21.9 1.2 gather_fusion
  23.2 1.2 gather_fusion
  24.4 1.2 gather_fusion
  25.6 1.2 gather_fusion
  28.1 1.2 gather_fusion
  29.4 1.2 gather_fusion
  30.6 6.8 %gather_fusion.2 = s32[1024]{0:T(1024)S(1)} fusion(s32[129]{0:T(256)S(1)} %convert_element_type.14, s32[1024]{0:T(1024)S(1)} %broadcast_clamp_fusion), kind=kCustom, calls=%fused_computation.2 | custom fusion | bytes 12288 | tf_op jit(solution)/shard_map/gather | solution.py:73
  37.4 4.3 %scatter_custom_fusion = s32[1024]{0:T(1024)S(1)} fusion(s32[1024]{0:T(1024)S(1)} %get-tuple-element.130, s32[1024]{0:T(1024)S(1)} %add_select_fusion.2, s32[]{:T(128)} %constant.80.clone.1), kind=kCustom, calls=%fused_computation.76 | custom fusion | bytes 4100 | tf_op jit(solution)/shard_map/scatter | solution.py:77
  41.8 4.3 %scatter_custom_fusion.1 = s32[1537]{0:T(1024)S(1)} fusion(s32[1024]{0:T(1024)S(1)} %get-tuple-element.126, s32[1024]{0:T(1024)S(1)} %get-tuple-element.127, s32[]{:T(128)} %constant.80.clone.1), kind=kCustom, calls=%fused_computation.66 | custom fusion | bytes 6152 | tf_op jit(solution)/shard_map/scatter | solution.py:78
  46.4 8.8 %all_to_all.20 = s32[4,1,384]{2,1,0:T(1,128)S(1)} all-to-all(s32[4,1,384]{2,1,0:T(1,128)S(1)} %reshape.175), channel_id=1, replica_groups=mesh['blk_0'=4,'blk_1'=8,'blk_2'=4,'rep'=2] {'blk_0'}, dimensions={0} | all-to-all | bytes 12288 | tf_op jit(solution)/shard_map/all_to_all | solution.py:37
  56.6 14.6 %all_to_all.21 = s32[8,1,192]{2,1,0:T(1,128)S(1)} all-to-all(s32[8,1,192]{2,1,0:T(1,128)S(1)} %reshape.177), channel_id=1, replica_groups=mesh['blk_0'=4,'blk_1'=8,'blk_2'=4,'rep'=2] {'blk_1'}, dimensions={0} | all-to-all | bytes 12288 | tf_op jit(solution)/shard_map/all_to_all | solution.py:37
  72.1 8.1 %all_to_all.22 = s32[4,1,384]{2,1,0:T(1,128)S(1)} all-to-all(s32[4,1,384]{2,1,0:T(1,128)S(1)} %reshape.179), channel_id=1, replica_groups=mesh['blk_0'=4,'blk_1'=8,'blk_2'=4,'rep'=2] {'blk_2'}, dimensions={0} | all-to-all | bytes 12288 | tf_op jit(solution)/shard_map/all_to_all | solution.py:37
  81.3 4.8 %gather_fusion.3 = bf16[1536,256]{1,0:T(8,128)(2,1)S(1)} fusion(bf16[2048,256]{1,0:T(8,128)(2,1)S(1)} %copy-done, s32[2048]{0:T(1024)S(1)} %pad_clamp_fusion.1), kind=kCustom, calls=%fused_computation.3 | custom fusion | bytes 1579008 | tf_op jit(solution)/shard_map/gather | solution.py:100
  87.2 6.2 %all-to-all-start.3 = ((bf16[128,12,256]{2,1,0:T(8,128)(2,1)}), bf16[128,12,256]{2,1,0:T(8,128)(2,1)S(1)}, u32[]{:S(2)}, u32[]{:S(2)}) async-start(bf16[128,12,256]{2,1,0:T(8,128)(2,1)} %reshape.113), calls=%async_computation.3 | async-start | bytes 2097152 | tf_op jit(solution)/shard_map/all_to_all | solution.py:101
  94.6 52.2 %all-reduce.9.cloned.1.call-done = f32[256,256]{1,0:T(8,128)} async-done(((f32[256,256]{1,0:T(8,128)}), f32[256,256]{1,0:T(8,128)}) %all-reduce.9.cloned.1.call-update) | async-done | bytes 262160 | tf_op jit(solution)/shard_map/psum | solution.py:17
  146.9 72.6 %all-reduce.11.cloned.1.call-done = f32[256,256]{1,0:T(8,128)} async-done(((f32[256,256]{1,0:T(8,128)}), f32[256,256]{1,0:T(8,128)}) %all-reduce.11.cloned.1.call-update) | async-done | bytes 262160 | tf_op jit(solution)/shard_map/psum | solution.py:17
  219.6 50.7 %all-reduce.13.cloned.1.call-done = f32[256,256]{1,0:T(8,128)} async-done(((f32[256,256]{1,0:T(8,128)}), f32[256,256]{1,0:T(8,128)}) %all-reduce.13.cloned.1.call-update) | async-done | bytes 262160 | tf_op jit(solution)/shard_map/psum | solution.py:17
  270.5 3.9 %gather_fusion.4 = bf16[1024,256]{1,0:T(8,128)(2,1)S(1)} fusion(bf16[1536,256]{1,0:T(8,128)(2,1)S(1)} %reshape.86, s32[1024]{0:T(1024)S(1)} %get-tuple-element.125), kind=kCustom, calls=%fused_computation.4 | custom fusion | bytes 1052672 | tf_op jit(solution)/shard_map/gather | solution.py:102
  276.4 28.7 %all-reduce.15.cloned.1.call-done = f32[256,256]{1,0:T(8,128)} async-done(((f32[256,256]{1,0:T(8,128)}), f32[256,256]{1,0:T(8,128)}) %all-reduce.15.cloned.1.call-update) | async-done | bytes 262160 | tf_op jit(solution)/shard_map/psum | solution.py:17
  312.2 1.3 multiply_reduce_fusion.4
  313.5 8.8 %all-reduce.2 = (f32[]{:T(128)}, f32[]{:T(128)}, f32[]{:T(128)}, f32[]{:T(128)}) all-reduce(f32[]{:T(128)} %get-tuple-element.93, f32[]{:T(128)} %get-tuple-element.92, f32[]{:T(128)} %get-tuple-element.90, f32[]{:T(128)} %get-tuple-element.87), channel_id=1, replica_groups=mesh['blk_0'=4,'blk_1'=8,'blk_2'=4,'rep'=2] {'blk_0'}, use_global_device_ids=true, to_apply=%region_31.32 | all-reduce | flops 4 | bytes 32 | tf_op jit(solution)/shard_map/psum | solution.py:17
  322.3 14.4 %all-reduce = (f32[]{:T(128)}, f32[]{:T(128)}, f32[]{:T(128)}, f32[]{:T(128)}) all-reduce(f32[]{:T(128)} %get-tuple-element.110, f32[]{:T(128)} %get-tuple-element.111, f32[]{:T(128)} %get-tuple-element.112, f32[]{:T(128)} %get-tuple-element.113), channel_id=1, replica_groups=mesh['blk_0'=4,'blk_1'=8,'blk_2'=4,'rep'=2] {'blk_1'}, use_global_device_ids=true, to_apply=%region_32.33 | all-reduce | flops 4 | bytes 32 | tf_op jit(solution)/shard_map/psum | solution.py:17
  336.7 9.1 %all-reduce.1 = (f32[]{:T(128)}, f32[]{:T(128)}, f32[]{:T(128)}, f32[]{:T(128)}) all-reduce(f32[]{:T(128)} %get-tuple-element.102, f32[]{:T(128)} %get-tuple-element.103, f32[]{:T(128)} %get-tuple-element.104, f32[]{:T(128)} %get-tuple-element.105), channel_id=1, replica_groups=mesh['blk_0'=4,'blk_1'=8,'blk_2'=4,'rep'=2] {'blk_2'}, use_global_device_ids=true, to_apply=%region_33.34 | all-reduce | flops 4 | bytes 32 | tf_op jit(solution)/shard_map/psum | solution.py:17
  345.9 10.9 %all-reduce.3 = (f32[1]{0:T(128)}, f32[1]{0:T(128)}, f32[1]{0:T(128)}, f32[1]{0:T(128)}) all-reduce(f32[1]{0:T(128)} %bitcast.36, f32[1]{0:T(128)} %bitcast.35, f32[1]{0:T(128)} %bitcast.34, f32[1]{0:T(128)} %bitcast.33), channel_id=1, replica_groups=mesh['blk_0'=4,'blk_1'=8,'blk_2'=4,'rep'=2] {'rep'}, use_global_device_ids=true, to_apply=%region_34.35 | all-reduce | flops 4 | bytes 32 | tf_op jit(solution)/shard_map/psum | solution.py:17
  356.7 3.0 fusion.29
  (109 shorter events, 17.4 us)
Async XLA Ops:
  7.2 74.1 %copy-start = (bf16[2048,256]{1,0:T(8,128)(2,1)S(1)}, bf16[2048,256]{1,0:T(8,128)(2,1)}, u32[]{:S(2)}) copy-start(bf16[2048,256]{1,0:T(8,128)(2,1)} %param.7) | copy-start | bytes 3145732
  87.2 183.1 %all-to-all-start.3 = ((bf16[128,12,256]{2,1,0:T(8,128)(2,1)}), bf16[128,12,256]{2,1,0:T(8,128)(2,1)S(1)}, u32[]{:S(2)}, u32[]{:S(2)}) async-start(bf16[128,12,256]{2,1,0:T(8,128)(2,1)} %reshape.113), calls=%async_computation.3 | async-start | bytes 2097152 | tf_op jit(solution)/shard_map/all_to_all | solution.py:101
  93.4 53.4 %all-reduce.9.cloned.1.call-start = ((), (), s32[]{:S(2)}) async-start(), calls=%async_computation.4 | async-start | bytes 524288 | tf_op jit(solution)/shard_map/psum | solution.py:17
  94.5 125.0 %all-reduce.11.cloned.1.call-start = ((), (), s32[]{:S(2)}) async-start(), calls=%async_computation.5 | async-start | bytes 524288 | tf_op jit(solution)/shard_map/psum | solution.py:17
  146.8 123.5 %all-reduce.13.cloned.1.call-start = ((), (), s32[]{:S(2)}) async-start(), calls=%async_computation.6 | async-start | bytes 524288 | tf_op jit(solution)/shard_map/psum | solution.py:17
  219.5 85.6 %all-reduce.15.cloned.1.call-start = ((), (), s32[]{:S(2)}) async-start(), calls=%async_computation.7 | async-start | bytes 524288 | tf_op jit(solution)/shard_map/psum | solution.py:17
  270.5 4.0 %copy-start.2 = (f32[8,256]{1,0:T(8,128)S(1)}, f32[8,256]{1,0:T(8,128)}, u32[]{:S(2)}) copy-start(f32[8,256]{1,0:T(8,128)} %param.8) | copy-start | bytes 24580
  274.5 0.7 copy-start.3
  275.0 0.7 copy-start.4
  306.9 1.0 copy-start.1
Sparse Core Ops, SparseCore 0:
  96.5 50.2 all-reduce.8
  149.1 70.3 all-reduce.10
  221.9 48.3 all-reduce.12
  272.7 32.3 all-reduce.14
where the time goes:
time: 367 us; the launch traced here: 366 us
  waiting for transfers between devices  204 us (56%)
  blocking collectives  74.7 us (20%)
  local copies, waits for them, and re-layouts  45.8 us (12%)
  between operations  14.1 us (4%)
  other arithmetic  13.2 us (4%)
  matrix products  7.29 us (2%)
  starting transfers between devices  6.35 us (2%)
    psum x4, waiting for transfers between devices, over_axes(): array = lax.psum(array, axis)  204 us
    psum x4, blocking collectives, over_axes(): array = lax.psum(array, axis)  43.2 us
    all_to_all x3, blocking collectives, moved_by_axis(): lax.all_to_all(pieces, axes[k], split_axis=k, concat_axis=k, tiled=True)  31.5 us
    gather x11, local copies, waits for them, and re-layouts, pack_requests(): jnp.searchsorted(sorted_owner, jnp.arange(blocks + 1, dtype=jnp.int32))  12.9 us
  transfers between devices with their start and end apart: 5, of which 4 were waited for; matrix products, arithmetic and copies ran while one was open for 2% of the time, Pallas kernels for 0%

commit v1 on v0

--- a/solution.py
+++ b/solution.py
@@ -14,7 +14,8 @@
 
 def over_axes(array, axes):
     for axis in axes:
-        array = lax.psum(array, axis)
+        parts = lax.all_gather(array, axis, axis=0, tiled=False)
+        array = parts.sum(axis=0)
     return array
 
 

time: 367 us -> 246 us (0.67)
  waiting for transfers between devices: 204 us -> 45.7 us
  local copies, waits for them, and re-layouts: 45.8 us -> 71.1 us
  other arithmetic: 13.2 us -> 28.9 us
    psum x4 -> x0, waiting for transfers between devices: 204 us -> none  [over_axes(): array = lax.psum(array, axis)]
    psum x4 -> x0, blocking collectives: 43.2 us -> none  [over_axes(): array = lax.psum(array, axis)]
    unnamed x0 -> x4, blocking collectives: none -> 38.7 us
    all_gather x0 -> x3, waiting for transfers between devices: none -> 27.4 us  [over_axes(): parts = lax.all_gather(array, axis, axis=0, tiled=False)]
    unnamed x17 -> x59, local copies, waits for them, and re-layouts: 2.05 us -> 27.4 us
    all_to_all x1, waiting for transfers between devices: 0.01 us -> 18.3 us  [body(): reply = lax.all_to_all(found, BLK, split_axis=0, concat_axis=0, tiled=True)]
    reduce_sum x0 -> x20, other arithmetic: none -> 15.6 us  [over_axes(): array = parts.sum(axis=0)]
    all_gather x0 -> x1, blocking collectives: none -> 4.2 us  [over_axes(): parts = lax.all_gather(array, axis, axis=0, tiled=False)]
  transfers between devices with their start and end apart: 5 -> 4, of which waited for: 4 -> 3; matrix products, arithmetic and copies ran while one was open for 2% -> 23% of each run, Pallas kernels for 0% -> 0%
where the time goes in v1:
time: 246 us; the launch traced here: 245 us
  blocking collectives  71.5 us (29%)
  local copies, waits for them, and re-layouts  71.1 us (29%)
  waiting for transfers between devices  45.7 us (19%)
  other arithmetic  28.9 us (12%)
  between operations  14.2 us (6%)
  starting transfers between devices  6.44 us (3%)
  matrix products  6.36 us (3%)
    unnamed x4, blocking collectives  38.7 us
    all_to_all x3, blocking collectives, moved_by_axis(): lax.all_to_all(pieces, axes[k], split_axis=k, concat_axis=k, tiled=True)  28.6 us
    unnamed x59, local copies, waits for them, and re-layouts  27.4 us
    all_gather x3, waiting for transfers between devices, over_axes(): parts = lax.all_gather(array, axis, axis=0, tiled=False)  27.4 us
    all_to_all x1, waiting for transfers between devices, body(): reply = lax.all_to_all(found, BLK, split_axis=0, concat_axis=0, tiled=True)  18.3 us
    reduce_sum x20, other arithmetic, over_axes(): array = parts.sum(axis=0)  15.6 us
    gather x11, local copies, waits for them, and re-layouts, pack_requests(): jnp.searchsorted(sorted_owner, jnp.arange(blocks + 1, dtype=jnp.int32))  12.9 us
    gather x1, local copies, waits for them, and re-layouts, pack_requests(): rank_sorted = jnp.arange(slot_total, dtype=jnp.int32) - starts[sorted_owner]  6.83 us
  transfers between devices with their start and end apart: 4, of which 3 were waited for; matrix products, arithmetic and copies ran while one was open for 23% of the time, Pallas kernels for 0%

profile of v1, /device:TPU:1, one launch (start us, length us, event | category | flops | bytes accessed | tf_op | source)
XLA Modules:
  0.0 244.6 jit_solution(10830549447623414149)
XLA Ops:
  10.2 4.4 %sort.17 = (s32[1024]{0:T(1024)}, s32[1024]{0:T(1024)S(1)}) sort(s32[1024]{0:T(1024)S(1)} %get-tuple-element.128, s32[1024]{0:T(1024)S(1)} %iota.14), dimensions={0}, to_apply=%region_0.0 | sort | flops 10240 | bytes 16384 | tf_op jit(solution)/shard_map/jit(argsort)/sort | solution.py:71
  14.6 4.5 %gather_fusion.1 = s32[1024]{0:T(1024)S(1)} fusion(s32[1024]{0:T(1024)S(1)} %get-tuple-element.128, s32[1024]{0:T(1024)S(1)} %get-tuple-element.129), kind=kCustom, calls=%fused_computation.1 | custom fusion | bytes 12288 | tf_op jit(solution)/shard_map/gather | solution.py:72
  19.2 19.0 %all-gather.8.cloned.1.call-done = f32[1024,256]{1,0:T(8,128)} async-done(((f32[256,256]{1,0:T(8,128)}), f32[1024,256]{1,0:T(8,128)}) %all-gather.8.cloned.1.call-update) | async-done | bytes 1048592 | tf_op jit(solution)/shard_map/all_gather | solution.py:17
  38.2 2.0 reduce_sum.274
  40.2 13.7 %while.24 = (s32[]{:T(128)}, u32[129]{0:T(256)S(1)}, u32[129]{0:T(256)S(1)}, s32[1024]{0:T(1024)S(1)}, s32[]{:T(128)}, /*index=5*/s32[]{:T(128)}, s32[]{}) while((s32[]{:T(128)}, u32[129]{0:T(256)S(1)}, u32[129]{0:T(256)S(1)}, s32[1024]{0:T(1024)S(1)}, s32[]{:T(128)}, /*index=5*/s32[]{:T(128)}, s32[]{}) %tuple.51), condition=%wide.region_2.0_spmd.clone, body=%wide.region_1.0_spmd.clone.sunk | while | flops 2705 | bytes 10396 | solution.py:73
  53.9 6.8 %gather_fusion.2 = s32[1024]{0:T(1024)S(1)} fusion(s32[129]{0:T(256)S(1)} %convert_element_type.14, s32[1024]{0:T(1024)S(1)} %broadcast_clamp_fusion), kind=kCustom, calls=%fused_computation.2 | custom fusion | bytes 12288 | tf_op jit(solution)/shard_map/gather | solution.py:74
  60.8 4.3 %scatter_custom_fusion = s32[1024]{0:T(1024)S(1)} fusion(s32[1024]{0:T(1024)S(1)} %get-tuple-element.130, s32[1024]{0:T(1024)S(1)} %add_select_fusion.2, s32[]{:T(128)} %constant.80.clone.1), kind=kCustom, calls=%fused_computation.76 | custom fusion | bytes 4100 | tf_op jit(solution)/shard_map/scatter | solution.py:78
  65.1 4.3 %scatter_custom_fusion.1 = s32[1537]{0:T(1024)S(1)} fusion(s32[1024]{0:T(1024)S(1)} %get-tuple-element.126, s32[1024]{0:T(1024)S(1)} %get-tuple-element.127, s32[]{:T(128)} %constant.80.clone.1), kind=kCustom, calls=%fused_computation.66 | custom fusion | bytes 6152 | tf_op jit(solution)/shard_map/scatter | solution.py:79
  69.7 7.7 %all_to_all.20 = s32[4,1,384]{2,1,0:T(1,128)S(1)} all-to-all(s32[4,1,384]{2,1,0:T(1,128)S(1)} %reshape.259), channel_id=1, replica_groups=mesh['blk_0'=4,'blk_1'=8,'blk_2'=4,'rep'=2] {'blk_0'}, dimensions={0} | all-to-all | bytes 12288 | tf_op jit(solution)/shard_map/all_to_all | solution.py:38
  78.8 13.0 %all_to_all.21 = s32[8,1,192]{2,1,0:T(1,128)S(1)} all-to-all(s32[8,1,192]{2,1,0:T(1,128)S(1)} %reshape.261), channel_id=1, replica_groups=mesh['blk_0'=4,'blk_1'=8,'blk_2'=4,'rep'=2] {'blk_1'}, dimensions={0} | all-to-all | bytes 12288 | tf_op jit(solution)/shard_map/all_to_all | solution.py:38
  92.8 8.0 %all_to_all.22 = s32[4,1,384]{2,1,0:T(1,128)S(1)} all-to-all(s32[4,1,384]{2,1,0:T(1,128)S(1)} %reshape.263), channel_id=1, replica_groups=mesh['blk_0'=4,'blk_1'=8,'blk_2'=4,'rep'=2] {'blk_2'}, dimensions={0} | all-to-all | bytes 12288 | tf_op jit(solution)/shard_map/all_to_all | solution.py:38
  101.7 4.8 %gather_fusion.3 = bf16[1536,256]{1,0:T(8,128)(2,1)S(1)} fusion(bf16[2048,256]{1,0:T(8,128)(2,1)S(1)} %copy-done, s32[2048]{0:T(1024)S(1)} %pad_clamp_fusion.1), kind=kCustom, calls=%fused_computation.3 | custom fusion | bytes 1579008 | tf_op jit(solution)/shard_map/gather | solution.py:101
  107.7 6.3 %all-to-all-start.3 = ((bf16[128,12,256]{2,1,0:T(8,128)(2,1)}), bf16[128,12,256]{2,1,0:T(8,128)(2,1)S(1)}, u32[]{:S(2)}, u32[]{:S(2)}) async-start(bf16[128,12,256]{2,1,0:T(8,128)(2,1)} %reshape.113), calls=%async_computation.3 | async-start | bytes 2097152 | tf_op jit(solution)/shard_map/all_to_all | solution.py:102
  114.1 2.5 %reduce_sum.275 = f32[256,256]{1,0:T(8,128)} reduce(f32[8,256,256]{2,1,0:T(8,128)} %bitcast.149, f32[]{:T(128)} %constant.79.clone.1), dimensions={0}, to_apply=%region_6.7 | reduce | flops 458752 | bytes 2359300 | tf_op jit(solution)/shard_map/reduce_sum | solution.py:18
  117.3 18.3 %all-to-all-done.3 = bf16[128,12,256]{2,1,0:T(8,128)(2,1)S(1)} async-done(((bf16[128,12,256]{2,1,0:T(8,128)(2,1)}), bf16[128,12,256]{2,1,0:T(8,128)(2,1)S(1)}, u32[]{:S(2)}, u32[]{:S(2)}) %all-to-all-start.3) | async-done | bytes 786464 | tf_op jit(solution)/shard_map/all_to_all | solution.py:102
  135.8 3.9 %gather_fusion.4 = bf16[1024,256]{1,0:T(8,128)(2,1)S(1)} fusion(bf16[1536,256]{1,0:T(8,128)(2,1)S(1)} %reshape.86, s32[1024]{0:T(1024)S(1)} %get-tuple-element.125), kind=kCustom, calls=%fused_computation.4 | custom fusion | bytes 1052672 | tf_op jit(solution)/shard_map/gather | solution.py:103
  140.9 8.3 %all-gather.12.cloned.1.call-done = f32[1024,256]{1,0:T(8,128)} async-done(((f32[256,256]{1,0:T(8,128)}), f32[1024,256]{1,0:T(8,128)}) %all-gather.12.cloned.1.call-update) | async-done | bytes 1048592 | tf_op jit(solution)/shard_map/all_gather | solution.py:17
  150.6 4.2 %all-gather.3 = f32[512,256]{1,0:T(8,128)S(1)} all-gather(f32[256,256]{1,0:T(8,128)S(1)} %reduce_sum.276), channel_id=5, replica_groups=mesh['blk_0'=4,'blk_1'=8,'blk_2'=4,'rep'=2] {'rep'}, dimensions={0}, use_global_device_ids=true | all-gather | bytes 786432 | tf_op jit(solution)/shard_map/all_gather | solution.py:17
  164.5 1.5 dynamic-update-slice.4
  166.0 1.4 dynamic-update-slice
  168.1 8.2 %all-reduce.18 = (f32[4]{0:T(128)S(1)}, f32[4]{0:T(128)S(1)}, f32[4]{0:T(128)S(1)}, f32[4]{0:T(128)S(1)}) all-reduce(f32[4]{0:T(128)S(1)} %dynamic-update-slice.12, f32[4]{0:T(128)S(1)} %dynamic-update-slice.8, f32[4]{0:T(128)S(1)} %dynamic-update-slice.4, ...), channel_id=1, replica_groups=mesh['blk_0'=4,'blk_1'=8,'blk_2'=4,'rep'=2] {'blk_0'}, use_global_device_ids=true, to_apply=%add.12 | all-reduce | flops 16 | bytes 128
  177.5 1.4 dynamic-update-slice.13
  180.9 1.4 dynamic-update-slice.5
  182.9 1.4 dynamic-update-slice.1
  185.0 13.3 %all-reduce.16 = (f32[8]{0:T(128)S(1)}, f32[8]{0:T(128)S(1)}, f32[8]{0:T(128)S(1)}, f32[8]{0:T(128)S(1)}) all-reduce(f32[8]{0:T(128)S(1)} %dynamic-update-slice.13, f32[8]{0:T(128)S(1)} %dynamic-update-slice.9, f32[8]{0:T(128)S(1)} %dynamic-update-slice.5, ...), channel_id=1, replica_groups=mesh['blk_0'=4,'blk_1'=8,'blk_2'=4,'rep'=2] {'blk_1'}, use_global_device_ids=true, to_apply=%add.13 | all-reduce | flops 32 | bytes 256
  199.5 1.4 dynamic-update-slice.14
  202.9 1.4 dynamic-update-slice.6
  207.1 6.9 %all-reduce.17 = (f32[4]{0:T(128)S(1)}, f32[4]{0:T(128)S(1)}, f32[4]{0:T(128)S(1)}, f32[4]{0:T(128)S(1)}) all-reduce(f32[4]{0:T(128)S(1)} %dynamic-update-slice.14, f32[4]{0:T(128)S(1)} %dynamic-update-slice.10, f32[4]{0:T(128)S(1)} %dynamic-update-slice.6, ...), channel_id=1, replica_groups=mesh['blk_0'=4,'blk_1'=8,'blk_2'=4,'rep'=2] {'blk_2'}, use_global_device_ids=true, to_apply=%add.14 | all-reduce | flops 16 | bytes 128
  215.2 1.4 dynamic-update-slice.15
  220.7 1.4 dynamic-update-slice.3
  222.1 10.3 %all-reduce.19 = (f32[2]{0:T(128)S(1)}, f32[2]{0:T(128)S(1)}, f32[2]{0:T(128)S(1)}, f32[2]{0:T(128)S(1)}) all-reduce(f32[2]{0:T(128)S(1)} %dynamic-update-slice.15, f32[2]{0:T(128)S(1)} %dynamic-update-slice.11, f32[2]{0:T(128)S(1)} %dynamic-update-slice.7, ...), channel_id=1, replica_groups=mesh['blk_0'=4,'blk_1'=8,'blk_2'=4,'rep'=2] {'rep'}, use_global_device_ids=true, to_apply=%add.15 | all-reduce | flops 8 | bytes 64
  235.0 3.1 %fusion.29 = f32[4]{0:T(128)} fusion(f32[1]{0:T(128)} %bitcast.60, f32[1]{0:T(128)} %bitcast.55, f32[1]{0:T(128)} %bitcast.50, f32[1]{0:T(128)} %bitcast.45), kind=kLoop, calls=%fused_computation.79 | loop fusion | flops 16 | bytes 32 | tf_op jit(solution)/shard_map/sqrt | solution.py:130
  (169 shorter events, 52.8 us)
Async XLA Ops:
  7.2 1.2 copy-start
  7.2 31.0 %all-gather.8.cloned.1.call-start = ((), (), s32[]{:S(2)}) async-start(), calls=%async_computation.4 | async-start | bytes 1310720 | tf_op jit(solution)/shard_map/all_gather | solution.py:17
  9.5 104.6 %all-gather.10.cloned.1.call-start = ((), (), s32[]{:S(2)}) async-start(), calls=%async_computation.5 | async-start | bytes 2359296 | tf_op jit(solution)/shard_map/all_gather | solution.py:17
  107.7 8.9 %copy-start.7 = (u32[256]{0:T(256)S(1)}, u32[256]{0:T(256)}, u32[]{:S(2)}) copy-start(u32[256]{0:T(256)} %constant.104) | copy-start | bytes 3076
  107.7 27.9 %all-to-all-start.3 = ((bf16[128,12,256]{2,1,0:T(8,128)(2,1)}), bf16[128,12,256]{2,1,0:T(8,128)(2,1)S(1)}, u32[]{:S(2)}, u32[]{:S(2)}) async-start(bf16[128,12,256]{2,1,0:T(8,128)(2,1)} %reshape.113), calls=%async_computation.3 | async-start | bytes 2097152 | tf_op jit(solution)/shard_map/all_to_all | solution.py:102
  114.0 35.3 %all-gather.12.cloned.1.call-start = ((), (), s32[]{:S(2)}) async-start(), calls=%async_computation.6 | async-start | bytes 1310720 | tf_op jit(solution)/shard_map/all_gather | solution.py:17
  135.7 4.0 %copy-start.1 = (f32[8,256]{1,0:T(8,128)S(1)}, f32[8,256]{1,0:T(8,128)}, u32[]{:S(2)}) copy-start(f32[8,256]{1,0:T(8,128)} %param.8) | copy-start | bytes 24580
  135.7 4.5 %copy-start.2 = (s32[8,128]{1,0:T(8,128)S(1)}, s32[8,128]{1,0:T(8,128)}, u32[]{:S(2)}) copy-start(s32[8,128]{1,0:T(8,128)} %param.11) | copy-start | bytes 12292
  135.7 4.5 %copy-start.3 = (s32[8]{0:T(128)S(1)}, s32[8]{0:T(128)}, u32[]{:S(2)}) copy-start(s32[8]{0:T(128)} %param.10) | copy-start | bytes 100
  155.1 12.4 %copy-start.6 = (u32[256]{0:T(256)S(1)}, u32[256]{0:T(256)}, u32[]{:S(2)}) copy-start(u32[256]{0:T(256)} %constant.109) | copy-start | bytes 3076
  155.1 29.3 %copy-start.5 = (u32[256]{0:T(256)S(1)}, u32[256]{0:T(256)}, u32[]{:S(2)}) copy-start(u32[256]{0:T(256)} %constant.114) | copy-start | bytes 3076
  155.1 51.3 %copy-start.4 = (u32[256]{0:T(256)S(1)}, u32[256]{0:T(256)}, u32[]{:S(2)}) copy-start(u32[256]{0:T(256)} %constant.119) | copy-start | bytes 3076
Sparse Core Ops, SparseCore 0:
  9.8 28.3 all-gather.7
  40.4 39.0 all-gather.9
  116.7 32.5 all-gather.11
